TPU v7x, 32 devices: a whole 2x2x4 slice. The times are simulated.
32 devices in a mesh: band: 8 (over z, core), lane: 4 (over y, x).
Axes of the slice: x: 2, y: 2, z: 4, core: 2. Of those that a mesh axis runs over, the one named last changes fastest.
Arguments:
- first_factor: bfloat16 [8192, 4096], P('band', 'lane'), may hold values from -6 to 6
- second_factor: bfloat16 [4096, 2048], P('band', 'lane'), may hold values from -0.09375 to 0.09375
- result_in: float32 [8192, 2048], P('band', 'lane'), may hold values from -6 to 6
- pivot_scale: float32 [4096], replicated, may hold values from 0.25 to 1.75
Outputs:
- updated: float32 [8192, 2048], P('band', 'lane')
All inputs are finite; a program needn't handle non-finite values.
Results may differ from a plain program's by a relative error of at most 0.002.
Values may be sent and summed in bfloat16 or wider, within the bound.
A program may use at most 128 MiB of HBM per device.

v0:
```python
import jax
import jax.numpy as jnp
from jax import lax
from jax.sharding import PartitionSpec as P


def join_panel(left_panel, right_panel):
    return jnp.dot(left_panel, right_panel, preferred_element_type=jnp.float32)


def on_device(first_factor, second_factor, result_in, pivot_scale):
    share = first_factor.shape[1]
    part_scale = lax.dynamic_slice_in_dim(pivot_scale, lax.axis_index("lane") * share, share)
    scaled_left = (first_factor.astype(jnp.float32) * part_scale).astype(jnp.bfloat16)
    left_line = lax.all_gather(scaled_left, "lane", axis=1, tiled=True)
    total = join_panel(left_line, lax.all_gather(second_factor, "band", axis=0, tiled=True))
    updated = result_in - total
    row_power = lax.psum(jnp.sum(updated * updated, axis=1), "lane")
    updated = (
        updated * lax.rsqrt(row_power / (updated.shape[1] * lax.axis_size("lane")) + 1e-06)[:, None]
    )
    return updated


def solution(mesh):
    return jax.shard_map(
        on_device,
        mesh=mesh,
        in_specs=(P("band", "lane"), P("band", "lane"), P("band", "lane"), P()),
        out_specs=P("band", "lane"),
        check_vma=False,
    )
```

profile of v0, /device:TPU:0, one launch (start us, length us, event | category | flops | bytes accessed | tf_op | source)
XLA Modules:
  0.0 177.2 jit_solution(5245780658395474004)
XLA Ops:
  6.5 0.0 all-gather.5.cloned.1.call-start
  6.5 0.7 all-gather.5.cloned.1.call-update
  7.3 0.0 all-gather.3.cloned.1.call-start
  7.3 0.7 dynamic_slice.3
  8.0 3.5 %multiply_convert_fusion = bf16[1024,1024]{1,0:T(8,128)(2,1)} fusion(bf16[1024,1024]{1,0:T(8,128)(2,1)} %param.4, f32[1024]{0:T(1024)S(1)} %dynamic_slice.3), kind=kLoop, calls=%fused_computation | loop fusion | flops 3145728 | bytes 4198400 | tf_op jit(solution)/shard_map/convert_element_type | solution.py:14
  11.5 0.0 copy-start
  11.5 0.0 all-gather.3.cloned.1.call-update
  11.5 1.6 copy-done
  13.1 1.8 %copy.5 = f32[1024,512]{0,1:T(8,128)} copy(f32[1024,512]{1,0:T(8,128)S(1)} %copy-done) | data formatting | bytes 4194304 | tf_op args[2]
  14.9 43.7 %all-gather.5.cloned.1.call-done = bf16[4096,512]{1,0:T(8,128)(2,1)} async-done(((bf16[512,512]{1,0:T(8,128)(2,1)}), bf16[4096,512]{1,0:T(8,128)(2,1)}) %all-gather.5.cloned.1.call-update) | async-done | bytes 4194320 | tf_op jit(solution)/shard_map/all_gather | solution.py:16
  58.6 88.2 %all-gather.3.cloned.1.call-done = bf16[1024,4096]{1,0:T(8,128)(2,1)} async-done(((bf16[1024,1024]{1,0:T(8,128)(2,1)}), bf16[1024,4096]{1,0:T(8,128)(2,1)}) %all-gather.3.cloned.1.call-update) | async-done | bytes 8388624 | tf_op jit(solution)/shard_map/all_gather | solution.py:15
  146.7 11.1 %multiply_reduce_fusion = (f32[1024]{0:T(1024)S(1)}, f32[1024,512]{0,1:T(8,128)}) fusion(f32[1024,512]{0,1:T(8,128)} %copy.5, bf16[1024,4096]{1,0:T(8,128)(2,1)} %all-gather.3.cloned.1.call-done, bf16[4096,512]{1,0:T(8,128)(2,1)} %all-gather.5.cloned.1.call-done), kind=kOutput, calls=%fused_computation.1 | convolution fusion | flops 4296539136 | bytes 16781312 | tf_op jit(solution)/shard_map/dot_general | solution.py:8
  157.8 8.9 %psum.7 = f32[1024]{0:T(1024)S(1)} all-reduce(f32[1024]{0:T(1024)S(1)} %get-tuple-element.5), channel_id=1, replica_groups=mesh['band'=8,'lane'=4] {'lane'}, use_global_device_ids=true, to_apply=%region_1.0 | all-reduce | flops 1024 | bytes 8192 | tf_op jit(solution)/shard_map/psum | solution.py:18
  166.7 1.8 %broadcast_multiply_fusion = f32[1024,512]{0,1:T(8,128)S(1)} fusion(f32[1024,512]{0,1:T(8,128)} %get-tuple-element.6, f32[1024]{0:T(1024)S(1)} %add_rsqrt_fusion), kind=kLoop, calls=%fused_computation.3 | loop fusion | flops 524288 | bytes 4198400 | tf_op jit(solution)/shard_map/mul | solution.py:20
  168.6 1.8 %copy.6 = f32[1024,512]{1,0:T(8,128)} copy(f32[1024,512]{0,1:T(8,128)S(1)} %broadcast_multiply_fusion) | data formatting | bytes 4194304 | tf_op jit(solution)/shard_map/mul | solution.py:20
  (1 shorter events, 0.0 us)
Async XLA Ops:
  6.5 52.0 %all-gather.5.cloned.1.call-start = ((), (), s32[]{:S(2)}) async-start(), calls=%async_computation.1 | async-start | bytes 4718592 | tf_op jit(solution)/shard_map/all_gather | solution.py:16
  7.3 139.5 %all-gather.3.cloned.1.call-start = ((), (), s32[]{:S(2)}) async-start(), calls=%async_computation | async-start | bytes 10485760 | tf_op jit(solution)/shard_map/all_gather | solution.py:15
  11.5 1.6 copy-start
Sparse Core Ops, SparseCore 0:
  8.9 49.5 all-gather.4
  60.4 86.2 all-gather.2
where the time goes:
time: 177 us
  waiting for transfers between devices  133 us (75%)
  between operations  13.4 us (8%)
  matrix products  11.1 us (6%)
  blocking collectives  8.9 us (5%)
  local copies, waits for them, and re-layouts  5.88 us (3%)
  other arithmetic  5.32 us (3%)
    all_gather x1, waiting for transfers between devices, on_device(): left_line = lax.all_gather(scaled_left, 'lane', axis=1, tiled=True)  88.2 us
    all_gather x1, waiting for transfers between devices, on_device(): lax.all_gather(second_factor, 'band', axis=0, tiled=True)  43.7 us
    dot_general x1, matrix products, join_panel(): return jnp.dot(left_panel, right_panel, preferred_element_type=jnp.float32)  11.1 us
    psum x1, blocking collectives, on_device(): row_power = lax.psum(jnp.sum(updated * updated, axis=1), 'lane')  8.9 us
  transfers between devices with their start and end apart: 2, of which 2 were waited for; matrix products, arithmetic and copies ran while one was open for 3% of the time, Pallas kernels for 0%

commit v1 on v0

--- a/solution.py
+++ b/solution.py
@@ -2,6 +2,19 @@
 import jax.numpy as jnp
 from jax import lax
 from jax.sharding import PartitionSpec as P
+
+
+def gather_around(x, axis, dim):
+    size, index, rows = (lax.axis_size(axis), lax.axis_index(axis), x.shape[dim])
+    ahead = [(i, (i + 1) % size) for i in range(size)]
+    out = jnp.zeros((*x.shape[:dim], size * rows, *x.shape[dim + 1 :]), x.dtype)
+    current = x
+    for turn in range(size):
+        owner = (index - turn) % size
+        out = lax.dynamic_update_slice_in_dim(out, current, owner * rows, axis=dim)
+        if turn < size - 1:
+            current = lax.ppermute(current, axis, ahead)
+    return out
 
 
 def join_panel(left_panel, right_panel):
@@ -13,7 +26,7 @@
     part_scale = lax.dynamic_slice_in_dim(pivot_scale, lax.axis_index("lane") * share, share)
     scaled_left = (first_factor.astype(jnp.float32) * part_scale).astype(jnp.bfloat16)
     left_line = lax.all_gather(scaled_left, "lane", axis=1, tiled=True)
-    total = join_panel(left_line, lax.all_gather(second_factor, "band", axis=0, tiled=True))
+    total = join_panel(left_line, gather_around(second_factor, "band", 0))
     updated = result_in - total
     row_power = lax.psum(jnp.sum(updated * updated, axis=1), "lane")
     updated = (

time: 177 us -> 131 us (0.74)
  waiting for transfers between devices: 133 us -> 74.5 us
  local copies, waits for them, and re-layouts: 5.88 us -> 17.9 us
    all_gather x1, waiting for transfers between devices: 88.2 us -> 13.3 us  [on_device(): left_line = lax.all_gather(scaled_left, 'lane', axis=1, tiled=True)]
    ppermute x0 -> x7, waiting for transfers between devices: none -> 61.2 us  [gather_around(): current = lax.ppermute(current, axis, ahead)]
    all_gather x1 -> x0, waiting for transfers between devices: 43.7 us -> none  [on_device(): lax.all_gather(second_factor, 'band', axis=0, tiled=True)]
    dynamic_update_slice x0 -> x8, local copies, waits for them, and re-layouts: none -> 8.78 us  [gather_around(): out = lax.dynamic_update_slice_in_dim(out, current, owner * rows, axis=dim)]
    broadcast_in_dim x0 -> x1, local copies, waits for them, and re-layouts: none -> 2.24 us  [gather_around(): out = jnp.zeros((*x.shape[:dim], size * rows, *x.shape[dim + 1:]), x.dtype)]
    unnamed x3 -> x19, local copies, waits for them, and re-layouts: 3.37 us -> 4.25 us
  transfers between devices with their start and end apart: 2 -> 8, of which waited for: 2 -> 8; matrix products, arithmetic and copies ran while one was open for 3% -> 10% of each run, Pallas kernels for 0% -> 0%
where the time goes in v1:
time: 131 us
  waiting for transfers between devices  74.5 us (57%)
  local copies, waits for them, and re-layouts  17.9 us (14%)
  between operations  13.4 us (10%)
  matrix products  10.4 us (8%)
  blocking collectives  8.9 us (7%)
  other arithmetic  5.41 us (4%)
    ppermute x7, waiting for transfers between devices, gather_around(): current = lax.ppermute(current, axis, ahead)  61.2 us
    all_gather x1, waiting for transfers between devices, on_device(): left_line = lax.all_gather(scaled_left, 'lane', axis=1, tiled=True)  13.3 us
    dot_general x1, matrix products, join_panel(): return jnp.dot(left_panel, right_panel, preferred_element_type=jnp.float32)  10.4 us
    psum x1, blocking collectives, on_device(): row_power = lax.psum(jnp.sum(updated * updated, axis=1), 'lane')  8.9 us
    dynamic_update_slice x8, local copies, waits for them, and re-layouts, gather_around(): out = lax.dynamic_update_slice_in_dim(out, current, owner * rows, axis=dim)  8.78 us
    unnamed x19, local copies, waits for them, and re-layouts  4.25 us
    convert_element_type x1, other arithmetic, on_device(): (first_factor.astype(jnp.float32) * part_scale).astype(jnp.bfloat16)  3.48 us
  transfers between devices with their start and end apart: 8, of which 8 were waited for; matrix products, arithmetic and copies ran while one was open for 10% of the time, Pallas kernels for 0%

profile of v1, /device:TPU:0, one launch (start us, length us, event | category | flops | bytes accessed | tf_op | source)
XLA Modules:
  0.0 131.2 jit_solution(17002306668225690973)
XLA Ops:
  6.5 0.0 copy-start.2
  6.5 0.0 copy-start
  6.5 0.0 all-gather.2.cloned.1.call-start
  6.5 0.8 dynamic_slice.3
  7.4 3.5 %multiply_convert_fusion = bf16[1024,1024]{1,0:T(8,128)(2,1)} fusion(bf16[1024,1024]{1,0:T(8,128)(2,1)} %param.4, f32[1024]{0:T(1024)S(1)} %dynamic_slice.3), kind=kLoop, calls=%fused_computation | loop fusion | flops 3145728 | bytes 4198400 | tf_op jit(solution)/shard_map/convert_element_type | solution.py:27
  10.9 0.0 all-gather.2.cloned.1.call-update
  10.9 0.0 copy-done.2
  10.9 0.5 collective-permute-start
  11.4 10.9 %collective-permute-done = bf16[512,512]{1,0:T(8,128)(2,1)S(1)} collective-permute-done((bf16[512,512]{1,0:T(8,128)(2,1)S(1)}, bf16[512,512]{1,0:T(8,128)(2,1)S(1)}, u32[]{:S(2)}, u32[]{:S(2)}) %collective-permute-start) | collective-permute-done | bytes 524320 | tf_op jit(solution)/shard_map/ppermute | solution.py:16
  22.3 0.0 copy-start.5
  22.3 0.0 collective-permute-start.1
  22.3 0.8 copy-done.5
  23.1 9.6 %collective-permute-done.1 = bf16[512,512]{1,0:T(8,128)(2,1)S(1)} collective-permute-done((bf16[512,512]{1,0:T(8,128)(2,1)S(1)}, bf16[512,512]{1,0:T(8,128)(2,1)S(1)}, u32[]{:S(2)}, u32[]{:S(2)}) %collective-permute-start.1) | collective-permute-done | bytes 524320 | tf_op jit(solution)/shard_map/ppermute | solution.py:16
  32.7 0.0 collective-permute-start.2
  32.7 10.4 %collective-permute-done.2 = bf16[512,512]{1,0:T(8,128)(2,1)S(1)} collective-permute-done((bf16[512,512]{1,0:T(8,128)(2,1)S(1)}, bf16[512,512]{1,0:T(8,128)(2,1)S(1)}, u32[]{:S(2)}, u32[]{:S(2)}) %collective-permute-start.2) | collective-permute-done | bytes 524320 | tf_op jit(solution)/shard_map/ppermute | solution.py:16
  43.1 0.0 copy-start.3
  43.1 0.8 copy-done.3
  44.0 0.0 collective-permute-start.3
  44.0 10.4 %collective-permute-done.3 = bf16[512,512]{1,0:T(8,128)(2,1)S(1)} collective-permute-done((bf16[512,512]{1,0:T(8,128)(2,1)S(1)}, bf16[512,512]{1,0:T(8,128)(2,1)S(1)}, u32[]{:S(2)}, u32[]{:S(2)}) %collective-permute-start.3) | collective-permute-done | bytes 524320 | tf_op jit(solution)/shard_map/ppermute | solution.py:16
  54.4 0.0 copy-start.7
  54.4 0.8 copy-done.7
  55.2 0.0 collective-permute-start.4
  55.2 10.5 %collective-permute-done.4 = bf16[512,512]{1,0:T(8,128)(2,1)} collective-permute-done((bf16[512,512]{1,0:T(8,128)(2,1)S(1)}, bf16[512,512]{1,0:T(8,128)(2,1)}, u32[]{:S(2)}, u32[]{:S(2)}) %collective-permute-start.4) | collective-permute-done | bytes 524320 | tf_op jit(solution)/shard_map/ppermute | solution.py:16
  65.7 0.0 collective-permute-start.5
  65.7 0.0 copy-done
  65.7 1.8 %copy.5 = f32[1024,512]{0,1:T(8,128)} copy(f32[1024,512]{1,0:T(8,128)S(1)} %copy-done) | data formatting | bytes 4194304 | tf_op args[2]
  67.5 0.0 copy-start.6
  67.5 2.2 %broadcast_in_dim.2 = bf16[4096,512]{1,0:T(8,128)(2,1)} broadcast(bf16[]{:T(256)} %constant.71.clone.1), dimensions={} | broadcast | bytes 4194306 | tf_op jit(solution)/shard_map/broadcast_in_dim | solution.py:10
  69.8 0.9 constant_dynamic-update-slice_fusion.7
  70.6 0.0 copy-done.6
  70.6 0.8 constant_dynamic-update-slice_fusion.6
  71.4 5.0 %collective-permute-done.5 = bf16[512,512]{1,0:T(8,128)(2,1)} collective-permute-done((bf16[512,512]{1,0:T(8,128)(2,1)}, bf16[512,512]{1,0:T(8,128)(2,1)}, u32[]{:S(2)}, u32[]{:S(2)}) %collective-permute-start.5) | collective-permute-done | bytes 524320 | tf_op jit(solution)/shard_map/ppermute | solution.py:16
  76.4 0.0 collective-permute-start.6
  76.4 0.8 constant_dynamic-update-slice_fusion.5
  77.3 0.0 copy-done.4
  77.3 0.8 constant_dynamic-update-slice_fusion.4
  78.1 0.0 copy-done.8
  78.1 0.8 constant_dynamic-update-slice_fusion.3
  78.9 1.9 %constant_dynamic-update-slice_fusion.2 = bf16[4096,512]{1,0:T(8,128)(2,1)} fusion(bf16[4096,512]{1,0:T(8,128)(2,1)} %constant_dynamic-update-slice_fusion.3, bf16[512,512]{1,0:T(8,128)(2,1)} %collective-permute-done.4, s32[]{:T(128)S(6)} %select_n.74), kind=kLoop, calls=%fused_computation.7 | loop fusion | bytes 1048580 | tf_op jit(solution)/shard_map/dynamic_update_slice | solution.py:14
  80.8 1.9 %constant_dynamic-update-slice_fusion.1 = bf16[4096,512]{1,0:T(8,128)(2,1)} fusion(bf16[4096,512]{1,0:T(8,128)(2,1)} %constant_dynamic-update-slice_fusion.2, bf16[512,512]{1,0:T(8,128)(2,1)} %collective-permute-done.5, s32[]{:T(128)S(6)} %select_n.76), kind=kLoop, calls=%fused_computation.6 | loop fusion | bytes 1048580 | tf_op jit(solution)/shard_map/dynamic_update_slice | solution.py:14
  82.7 4.4 %collective-permute-done.6 = bf16[512,512]{1,0:T(8,128)(2,1)S(1)} collective-permute-done((bf16[512,512]{1,0:T(8,128)(2,1)}, bf16[512,512]{1,0:T(8,128)(2,1)S(1)}, u32[]{:S(2)}, u32[]{:S(2)}) %collective-permute-start.6) | collective-permute-done | bytes 524320 | tf_op jit(solution)/shard_map/ppermute | solution.py:16
  87.0 0.9 constant_dynamic-update-slice_fusion
  87.9 13.3 %all-gather.2.cloned.1.call-done = bf16[1024,4096]{1,0:T(8,128)(2,1)} async-done(((bf16[1024,1024]{1,0:T(8,128)(2,1)}), bf16[1024,4096]{1,0:T(8,128)(2,1)}) %all-gather.2.cloned.1.call-update) | async-done | bytes 8388624 | tf_op jit(solution)/shard_map/all_gather | solution.py:28
  101.2 0.0 copy-done.1
  101.2 10.4 %multiply_reduce_fusion = (f32[1024]{0:T(1024)S(1)}, f32[1024,512]{0,1:T(8,128)}) fusion(f32[1024,512]{0,1:T(8,128)S(1)} %copy-done.1, bf16[1024,4096]{1,0:T(8,128)(2,1)} %all-gather.2.cloned.1.call-done, bf16[4096,512]{1,0:T(8,128)(2,1)} %constant_dynamic-update-slice_fusion), kind=kOutput, calls=%fused_computation.1 | convolution fusion | flops 4296539136 | bytes 16781312 | tf_op jit(solution)/shard_map/dot_general | solution.py:21
  111.7 8.9 %psum.7 = f32[1024]{0:T(1024)S(1)} all-reduce(f32[1024]{0:T(1024)S(1)} %get-tuple-element.5), channel_id=1, replica_groups=mesh['band'=8,'lane'=4] {'lane'}, use_global_device_ids=true, to_apply=%region_1.2 | all-reduce | flops 1024 | bytes 8192 | tf_op jit(solution)/shard_map/psum | solution.py:31
  120.6 1.9 %broadcast_multiply_fusion = f32[1024,512]{0,1:T(8,128)S(1)} fusion(f32[1024,512]{0,1:T(8,128)} %get-tuple-element.6, f32[1024]{0:T(1024)S(1)} %add_rsqrt_fusion), kind=kLoop, calls=%fused_computation.3 | loop fusion | flops 524288 | bytes 4198400 | tf_op jit(solution)/shard_map/mul | solution.py:33
  122.5 1.8 %copy.6 = f32[1024,512]{1,0:T(8,128)} copy(f32[1024,512]{0,1:T(8,128)S(1)} %broadcast_multiply_fusion) | data formatting | bytes 4194304 | tf_op jit(solution)/shard_map/mul | solution.py:33
  (4 shorter events, 0.0 us)
Async XLA Ops:
  6.5 4.4 %copy-start.2 = (bf16[512,512]{1,0:T(8,128)(2,1)S(1)}, bf16[512,512]{1,0:T(8,128)(2,1)}, u32[]{:S(2)}) copy-start(bf16[512,512]{1,0:T(8,128)(2,1)} %param.5) | copy-start | bytes 1572868
  6.5 59.2 %copy-start = (f32[1024,512]{1,0:T(8,128)S(1)}, f32[1024,512]{1,0:T(8,128)}, u32[]{:S(2)}) copy-start(f32[1024,512]{1,0:T(8,128)} %param.6) | copy-start | bytes 6291460
  6.5 94.7 %all-gather.2.cloned.1.call-start = ((), (), s32[]{:S(2)}) async-start(), calls=%async_computation | async-start | bytes 10485760 | tf_op jit(solution)/shard_map/all_gather | solution.py:28
  10.9 11.4 %collective-permute-start = (bf16[512,512]{1,0:T(8,128)(2,1)S(1)}, bf16[512,512]{1,0:T(8,128)(2,1)S(1)}, u32[]{:S(2)}, u32[]{:S(2)}) collective-permute-start(bf16[512,512]{1,0:T(8,128)(2,1)S(1)} %copy-done.2), channel_id=1, source_target_pairs={{0,4},{4,8},{8,12},{12,16},{16,20},{20,24},{24,28},{28,0},{1,5},{5... | collective-permute-start | bytes 1572872 | tf_op jit(solution)/shard_map/ppermute | solution.py:16
  22.3 0.8 copy-start.5
  22.3 10.4 %collective-permute-start.1 = (bf16[512,512]{1,0:T(8,128)(2,1)S(1)}, bf16[512,512]{1,0:T(8,128)(2,1)S(1)}, u32[]{:S(2)}, u32[]{:S(2)}) collective-permute-start(bf16[512,512]{1,0:T(8,128)(2,1)S(1)} %collective-permute-done), channel_id=1, source_target_pairs={{0,4},{4,8},{8,12},{12,16},{16,20},{20,24},{24,28},{28,0},{1,5},{5... | collective-permute-start | bytes 1572872 | tf_op jit(solution)/shard_map/ppermute | solution.py:16
  32.7 10.4 %collective-permute-start.2 = (bf16[512,512]{1,0:T(8,128)(2,1)S(1)}, bf16[512,512]{1,0:T(8,128)(2,1)S(1)}, u32[]{:S(2)}, u32[]{:S(2)}) collective-permute-start(bf16[512,512]{1,0:T(8,128)(2,1)S(1)} %collective-permute-done.1), channel_id=1, source_target_pairs={{0,4},{4,8},{8,12},{12,16},{16,20},{20,24},{24,28},{28,0},{1,5},{5... | collective-permute-start | bytes 1572872 | tf_op jit(solution)/shard_map/ppermute | solution.py:16
  43.1 0.8 copy-start.3
  44.0 10.4 %collective-permute-start.3 = (bf16[512,512]{1,0:T(8,128)(2,1)S(1)}, bf16[512,512]{1,0:T(8,128)(2,1)S(1)}, u32[]{:S(2)}, u32[]{:S(2)}) collective-permute-start(bf16[512,512]{1,0:T(8,128)(2,1)S(1)} %collective-permute-done.2), channel_id=1, source_target_pairs={{0,4},{4,8},{8,12},{12,16},{16,20},{20,24},{24,28},{28,0},{1,5},{5... | collective-permute-start | bytes 1572872 | tf_op jit(solution)/shard_map/ppermute | solution.py:16
  54.4 0.8 copy-start.7
  55.2 10.5 %collective-permute-start.4 = (bf16[512,512]{1,0:T(8,128)(2,1)S(1)}, bf16[512,512]{1,0:T(8,128)(2,1)}, u32[]{:S(2)}, u32[]{:S(2)}) collective-permute-start(bf16[512,512]{1,0:T(8,128)(2,1)S(1)} %collective-permute-done.3), channel_id=1, source_target_pairs={{0,4},{4,8},{8,12},{12,16},{16,20},{20,24},{24,28},{28,0},{1,5},{5... | collective-permute-start | bytes 1572872 | tf_op jit(solution)/shard_map/ppermute | solution.py:16
  65.7 10.7 %collective-permute-start.5 = (bf16[512,512]{1,0:T(8,128)(2,1)}, bf16[512,512]{1,0:T(8,128)(2,1)}, u32[]{:S(2)}, u32[]{:S(2)}) collective-permute-start(bf16[512,512]{1,0:T(8,128)(2,1)} %collective-permute-done.4), channel_id=1, source_target_pairs={{0,4},{4,8},{8,12},{12,16},{16,20},{20,24},{24,28},{28,0},{1,5},{5... | collective-permute-start | bytes 1572872 | tf_op jit(solution)/shard_map/ppermute | solution.py:16
  67.5 3.1 %copy-start.6 = (bf16[512,512]{1,0:T(8,128)(2,1)S(1)}, bf16[512,512]{1,0:T(8,128)(2,1)}, u32[]{:S(2)}) copy-start(bf16[512,512]{1,0:T(8,128)(2,1)} %copy-done.5) | copy-start | bytes 1572868
  67.5 9.7 %copy-start.4 = (bf16[512,512]{1,0:T(8,128)(2,1)S(1)}, bf16[512,512]{1,0:T(8,128)(2,1)}, u32[]{:S(2)}) copy-start(bf16[512,512]{1,0:T(8,128)(2,1)} %copy-done.3) | copy-start | bytes 1572868
  67.5 10.6 %copy-start.8 = (bf16[512,512]{1,0:T(8,128)(2,1)S(1)}, bf16[512,512]{1,0:T(8,128)(2,1)}, u32[]{:S(2)}) copy-start(bf16[512,512]{1,0:T(8,128)(2,1)} %copy-done.7) | copy-start | bytes 1572868
  69.8 31.5 %copy-start.1 = (f32[1024,512]{0,1:T(8,128)S(1)}, f32[1024,512]{0,1:T(8,128)}, u32[]{:S(2)}) copy-start(f32[1024,512]{0,1:T(8,128)} %copy.5) | copy-start | bytes 6291460
  76.4 10.6 %collective-permute-start.6 = (bf16[512,512]{1,0:T(8,128)(2,1)}, bf16[512,512]{1,0:T(8,128)(2,1)S(1)}, u32[]{:S(2)}, u32[]{:S(2)}) collective-permute-start(bf16[512,512]{1,0:T(8,128)(2,1)} %collective-permute-done.5), channel_id=1, source_target_pairs={{0,4},{4,8},{8,12},{12,16},{16,20},{20,24},{24,28},{28,0},{1,5},{5... | collective-permute-start | bytes 1572872 | tf_op jit(solution)/shard_map/ppermute | solution.py:16
Sparse Core Ops, SparseCore 0:
  11.0 90.1 all-gather.1
